TPU v7x, 32 devices: a whole 2x2x4 slice. The times are simulated.
32 devices in a mesh: space: 16 (over z, y, core), tm: 2 (over x).
Axes of the slice: x: 2, y: 2, z: 4, core: 2. Of those that a mesh axis runs over, the one named last changes fastest.
Arguments:
- solutions: bfloat16 [2, 12, 8192, 128], P('tm', None, 'space'), may hold values from -6 to 6
- noise: int32 [2, 64, 12, 8192], P('tm', None, None, 'space'), may hold values from 0 to 3
- momenta: int32 [27, 3], replicated, may hold values from -2 to 2
- pairs: int32 [16, 2], P('tm'), may hold values from 0 to 1
Outputs:
- mesons: float32 [2, 2, 27, 64, 64], P('tm', None, None, 'space')
- correlators: float32 [16, 2, 27], P('tm')
All inputs are finite; a program needn't handle non-finite values.
Results may differ from a plain program's by a relative error of at most 0.002.
Values sent between devices are 32-bit elements; how exact they have to be, the bound alone decides.
A program may use at most 64 MiB of HBM per device.

v0:
```python
import math

import jax
import jax.numpy as jnp
from jax import lax
from jax.sharding import PartitionSpec as P

EXTENT = 48


def phase_weights(noise_block, momenta, coords):
    qdotx = (
        momenta[:, 0:1] * coords[0][None, :]
        + momenta[:, 1:2] * coords[1][None, :]
        + momenta[:, 2:3] * coords[2][None, :]
    )
    base_index = qdotx % EXTENT
    angle = base_index.astype(jnp.float32) * jnp.float32(2.0 * math.pi / EXTENT)
    base_re = jnp.cos(angle).astype(jnp.bfloat16)[:, None, None, :]
    base_im = (-jnp.sin(angle)).astype(jnp.bfloat16)[:, None, None, :]
    turns = (noise_block % 4)[None, :, :, :]
    weight_re = jnp.where(
        turns == 0,
        base_re,
        jnp.where(turns == 1, base_im, jnp.where(turns == 2, -base_re, -base_im)),
    )
    weight_im = jnp.where(
        turns == 0,
        base_im,
        jnp.where(turns == 1, -base_re, jnp.where(turns == 2, -base_im, base_re)),
    )
    rows = momenta.shape[0] * noise_block.shape[0]
    cols = noise_block.shape[1] * noise_block.shape[2]
    return (weight_re.reshape(rows, cols), weight_im.reshape(rows, cols))


def partial_field(vectors, sources, momenta, offset):
    spincol, sites, width = vectors.shape
    nvec = width // 2
    moms = momenta.shape[0]
    block = min(128, sites)
    nblocks = sites // block

    def one_block(step, total):
        first = (step * block).astype(jnp.int32)
        noise_block = lax.dynamic_slice_in_dim(sources, first, block, 2)
        vec_block = lax.dynamic_slice_in_dim(vectors, first, block, 1)
        glob = offset + first + jnp.arange(block, dtype=jnp.int32)
        coords = (glob % EXTENT, glob // EXTENT % EXTENT, glob // (EXTENT * EXTENT))
        weight_re, weight_im = phase_weights(noise_block, momenta, coords)
        stacked = vec_block.reshape(spincol * block, width)
        left = jnp.dot(weight_re, stacked, preferred_element_type=jnp.float32)
        right = jnp.dot(weight_im, stacked, preferred_element_type=jnp.float32)
        real_part = left[:, :nvec] - right[:, nvec:]
        imag_part = left[:, nvec:] + right[:, :nvec]
        return total + jnp.stack([real_part, imag_part], 0)

    start = jnp.zeros((2, moms * nvec, nvec), jnp.float32)
    total = lax.fori_loop(0, nblocks, one_block, start)
    return total.reshape(2, moms, nvec, nvec)


def pair_traces(fields, pairs):
    nslices = fields.shape[0]
    slots = jnp.arange(nslices, dtype=jnp.int32)
    pick_sink = (pairs[:, 1][:, None] == slots[None, :]).astype(jnp.float32)
    pick_source = (pairs[:, 0][:, None] == slots[None, :]).astype(jnp.float32)
    sink = jnp.einsum("kt,tcpij->kcpij", pick_sink, fields, precision=lax.Precision.HIGHEST)
    source = jnp.einsum("kt,tcpij->kcpij", pick_source, fields, precision=lax.Precision.HIGHEST)
    real_part = jnp.sum(sink[:, 0] * source[:, 0] + sink[:, 1] * source[:, 1], axis=(2, 3))
    imag_part = jnp.sum(sink[:, 1] * source[:, 0] - sink[:, 0] * source[:, 1], axis=(2, 3))
    return jnp.stack([real_part, imag_part], 1)


def local(solutions, noise, momenta, pairs):
    slice_count, spincol, sites_local, width = solutions.shape
    nvec = width // 2
    nspace = lax.axis_size("space")
    scale = 1.0 / math.sqrt(spincol * sites_local * nspace)
    offset = lax.axis_index("space") * sites_local
    terms = jnp.stack([partial_field(solutions[0], noise[0], momenta, offset) * scale], 0)
    mesons = lax.psum_scatter(terms, "space", scatter_dimension=3, tiled=True)
    every_slice = lax.all_gather(mesons, "tm", axis=0, tiled=True)
    partial_traces = pair_traces(every_slice, pairs)
    correlators = lax.psum(partial_traces, "space") / nvec
    return (mesons, correlators)


def solution(mesh):
    in_specs = (P("tm", None, "space", None), P("tm", None, None, "space"), P(), P("tm", None))
    out_specs = (P("tm", None, None, "space", None), P("tm", None, None))
    return jax.shard_map(local, mesh=mesh, in_specs=in_specs, out_specs=out_specs, check_vma=False)
```

profile of v0, /device:TPU:0, one launch (start us, length us, event | category | flops | bytes accessed | tf_op | source)
XLA Modules:
  0.0 223.5 jit_solution(1606789766485243148)
XLA Ops:
  7.2 0.0 copy-start.1
  7.2 0.0 all-reduce.3.cloned.1.call-start
  7.2 3.7 %copy.53 = s32[1,64,12,512]{3,2,1,0:T(8,128)} copy(s32[1,64,12,512]{3,1,2,0:T(8,128)} %param.7) | data formatting | bytes 3145728 | tf_op args[1]
  11.0 0.0 copy-done.1
  11.0 64.5 %while.17 = (s32[]{:T(128)}, f32[2,1728,64]{2,1,0:T(8,128)S(1)}, s32[64,12,512]{2,1,0:T(8,128)}, s32[27,3]{0,1:T(4,128)S(1)}, s32[]{:T(128)}, /*index=5*/bf16[12...) while((s32[]{:T(128)}, f32[2,1728,64]{2,1,0:T(8,128)S(1)}, ...), condition=%wide.region_1.2_spmd.clone, body=%wide.region_0.1_spmd.clone.sunk | while | flops 1377275648 | bytes 30928840 | solution.py:59
  11.0 0.2 fusion.44
  11.2 0.2 cosine_convert_fusion.2
  11.4 1.4 broadcast_compare_fusion.4
  12.8 6.0 %select_select_fusion.3 = (bf16[27,64,12,128]{3,2,1,0:T(8,128)(2,1)}, bf16[27,64,12,128]{3,2,1,0:T(8,128)(2,1)S(1)}) fusion(pred[64,12,128]{2,1,0:T(8,128)(4,1)S(1)} %get-tuple-element.309, pred[64,12,128]{2,1,0:T(8,128)(4,1)S(1)} %get-tuple-element.310, pred[64,12,128]{2,1,0:T(8,128)(4,1)S(1)} %get-tuple-element.311, ...), kind=kLoop, calls=%fused_computation.1.clone.1 | loop fusion | flops 15925248 | bytes 10939392 | tf_op jit(solution)/shard_map/while/body/eval_jaxpr/jit(_where)/select_n | solution.py:22
  18.8 1.0 constant_dynamic-slice_fusion.3
  19.8 4.6 %fusion.46 = f32[1728,128]{1,0:T(8,128)S(1)} fusion(bf16[1536,128]{1,0:T(8,128)(2,1)S(1)} %bitcast.66, bf16[216,8,12,128]{3,2,1,0:T(8,128)(2,1)} %bitcast.64), kind=kOutput, calls=%fused_computation.5.clone.1 | convolution fusion | flops 679477248 | bytes 6586368 | tf_op jit(solution)/shard_map/while/body/eval_jaxpr/dot_general | solution.py:52
  24.4 1.6 fusion.45
  26.0 0.5 fusion.47
  26.5 0.6 maximum_add_fusion.2
  27.2 0.2 fusion.44
  27.3 0.2 cosine_convert_fusion.2
  27.5 1.4 broadcast_compare_fusion.4
  29.0 6.0 %select_select_fusion.3 = (bf16[27,64,12,128]{3,2,1,0:T(8,128)(2,1)}, bf16[27,64,12,128]{3,2,1,0:T(8,128)(2,1)S(1)}) fusion(pred[64,12,128]{2,1,0:T(8,128)(4,1)S(1)} %get-tuple-element.309, pred[64,12,128]{2,1,0:T(8,128)(4,1)S(1)} %get-tuple-element.310, pred[64,12,128]{2,1,0:T(8,128)(4,1)S(1)} %get-tuple-element.311, ...), kind=kLoop, calls=%fused_computation.1.clone.1 | loop fusion | flops 15925248 | bytes 10939392 | tf_op jit(solution)/shard_map/while/body/eval_jaxpr/jit(_where)/select_n | solution.py:22
  34.9 1.0 constant_dynamic-slice_fusion.3
  35.9 4.6 %fusion.46 = f32[1728,128]{1,0:T(8,128)S(1)} fusion(bf16[1536,128]{1,0:T(8,128)(2,1)S(1)} %bitcast.66, bf16[216,8,12,128]{3,2,1,0:T(8,128)(2,1)} %bitcast.64), kind=kOutput, calls=%fused_computation.5.clone.1 | convolution fusion | flops 679477248 | bytes 6586368 | tf_op jit(solution)/shard_map/while/body/eval_jaxpr/dot_general | solution.py:52
  40.5 1.6 fusion.45
  42.1 0.5 fusion.47
  42.6 0.6 maximum_add_fusion.2
  43.3 0.2 fusion.44
  43.5 0.2 cosine_convert_fusion.2
  43.6 1.4 broadcast_compare_fusion.4
  45.1 6.0 %select_select_fusion.3 = (bf16[27,64,12,128]{3,2,1,0:T(8,128)(2,1)}, bf16[27,64,12,128]{3,2,1,0:T(8,128)(2,1)S(1)}) fusion(pred[64,12,128]{2,1,0:T(8,128)(4,1)S(1)} %get-tuple-element.309, pred[64,12,128]{2,1,0:T(8,128)(4,1)S(1)} %get-tuple-element.310, pred[64,12,128]{2,1,0:T(8,128)(4,1)S(1)} %get-tuple-element.311, ...), kind=kLoop, calls=%fused_computation.1.clone.1 | loop fusion | flops 15925248 | bytes 10939392 | tf_op jit(solution)/shard_map/while/body/eval_jaxpr/jit(_where)/select_n | solution.py:22
  51.0 1.0 constant_dynamic-slice_fusion.3
  52.1 4.6 %fusion.46 = f32[1728,128]{1,0:T(8,128)S(1)} fusion(bf16[1536,128]{1,0:T(8,128)(2,1)S(1)} %bitcast.66, bf16[216,8,12,128]{3,2,1,0:T(8,128)(2,1)} %bitcast.64), kind=kOutput, calls=%fused_computation.5.clone.1 | convolution fusion | flops 679477248 | bytes 6586368 | tf_op jit(solution)/shard_map/while/body/eval_jaxpr/dot_general | solution.py:52
  56.7 1.6 fusion.45
  58.2 0.5 fusion.47
  58.8 0.6 maximum_add_fusion.2
  59.4 0.2 fusion.44
  59.6 0.2 cosine_convert_fusion.2
  59.8 1.4 broadcast_compare_fusion.4
  61.2 6.0 %select_select_fusion.3 = (bf16[27,64,12,128]{3,2,1,0:T(8,128)(2,1)}, bf16[27,64,12,128]{3,2,1,0:T(8,128)(2,1)S(1)}) fusion(pred[64,12,128]{2,1,0:T(8,128)(4,1)S(1)} %get-tuple-element.309, pred[64,12,128]{2,1,0:T(8,128)(4,1)S(1)} %get-tuple-element.310, pred[64,12,128]{2,1,0:T(8,128)(4,1)S(1)} %get-tuple-element.311, ...), kind=kLoop, calls=%fused_computation.1.clone.1 | loop fusion | flops 15925248 | bytes 10939392 | tf_op jit(solution)/shard_map/while/body/eval_jaxpr/jit(_where)/select_n | solution.py:22
  67.2 1.0 constant_dynamic-slice_fusion.3
  68.2 4.6 %fusion.46 = f32[1728,128]{1,0:T(8,128)S(1)} fusion(bf16[1536,128]{1,0:T(8,128)(2,1)S(1)} %bitcast.66, bf16[216,8,12,128]{3,2,1,0:T(8,128)(2,1)} %bitcast.64), kind=kOutput, calls=%fused_computation.5.clone.1 | convolution fusion | flops 679477248 | bytes 6586368 | tf_op jit(solution)/shard_map/while/body/eval_jaxpr/dot_general | solution.py:52
  72.8 1.6 fusion.45
  74.4 0.5 fusion.47
  74.9 0.6 maximum_add_fusion.2
  75.5 0.2 broadcast_multiply_fusion
  75.6 0.0 copy-start.3
  75.7 0.0 copy-start.2
  75.7 2.6 %copy.26 = f32[1,2,27,64,64]{4,1,2,0,3:T(2,128)} copy(f32[1,2,27,64,64]{4,3,2,1,0:T(8,128)S(1)} %bitcast.68) | data formatting | bytes 1769472 | tf_op jit(solution)/shard_map/mul | solution.py:81
  78.2 0.0 all-reduce.3.cloned.1.call-update
  78.3 0.0 copy-done.3
  78.3 0.6 dynamic-slice
  79.5 0.0 copy-done.2
  79.5 98.4 %all-reduce.3.cloned.1.call-done = f32[1,2,27,64,64]{4,1,2,0,3:T(2,128)} async-done(((f32[1,2,27,64,64]{4,1,2,0,3:T(2,128)}), f32[1,2,27,64,64]{4,1,2,0,3:T(2,128)}) %all-reduce.3.cloned.1.call-update) | async-done | bytes 884752
  177.9 0.9 constant_dynamic-slice_fusion.1
  178.9 0.0 copy-start
  178.9 5.4 %all_gather.3 = f32[2,2,27,4,64]{4,3,2,1,0:T(4,128)S(1)} all-gather(f32[1,2,27,4,64]{4,3,2,1,0:T(4,128)S(1)} %copy.32), channel_id=1, replica_groups=mesh['space'=16,'tm'=2] {'tm'}, dimensions={0}, use_global_device_ids=true | all-gather | bytes 165888 | tf_op jit(solution)/shard_map/all_gather | solution.py:83
  184.3 0.7 fusion.18
  185.0 0.7 fusion.20
  185.6 0.2 add_reduce_fusion
  185.9 0.0 copy-done
  185.9 0.1 copy.30
  185.9 0.1 copy.31
  186.0 30.0 %psum.7 = f32[8,2,27]{2,0,1:T(8,128)S(1)} all-reduce(f32[8,2,27]{2,0,1:T(8,128)S(1)} %pad_maximum_fusion), channel_id=1, replica_groups=mesh['space'=16,'tm'=2] {'space'}, use_global_device_ids=true, to_apply=%region_5.6 | all-reduce | flops 432 | bytes 3456 | tf_op jit(solution)/shard_map/psum | solution.py:85
  216.0 0.6 copy.33
  (17 shorter events, 0.2 us)
Async XLA Ops:
  7.2 3.8 %copy-start.1 = (s32[27,3]{0,1:T(4,128)S(1)}, s32[27,3]{0,1:T(4,128)}, u32[]{:S(2)}) copy-start(s32[27,3]{0,1:T(4,128)} %param.8) | copy-start | bytes 976
  7.2 170.8 %all-reduce.3.cloned.1.call-start = ((), (), s32[]{:S(2)}) async-start(), calls=%async_computation | async-start | bytes 3538944
  75.6 2.6 %copy-start.3 = (u32[32]{0:T(128)S(1)}, u32[32]{0:T(128)}, u32[]{:S(2)}) copy-start(u32[32]{0:T(128)} %constant.167) | copy-start | bytes 388
  75.7 3.9 %copy-start.2 = (s32[8,2]{0,1:T(2,128)S(1)}, s32[8,2]{0,1:T(2,128)}, u32[]{:S(2)}) copy-start(s32[8,2]{0,1:T(2,128)} %param.9) | copy-start | bytes 196
  178.9 7.0 %copy-start = (f32[1,2,27,4,64]{4,3,2,1,0:T(4,128)}, f32[1,2,27,4,64]{4,3,2,1,0:T(4,128)S(1)}, u32[]{:S(2)}) copy-start(f32[1,2,27,4,64]{4,3,2,1,0:T(4,128)S(1)} %copy.32) | copy-start | bytes 165892
Sparse Core Ops, SparseCore 0:
  78.4 99.5 all-reduce.2
where the time goes:
time: 224 us; the launch traced here: 223 us
  waiting for transfers between devices  98.4 us (44%)
  other arithmetic  35.8 us (16%)
  blocking collectives  35.4 us (16%)
  matrix products  25.9 us (12%)
  between operations  14.8 us (7%)
  local copies, waits for them, and re-layouts  12.7 us (6%)
    unnamed x2, waiting for transfers between devices  98.4 us
    psum x1, blocking collectives, local(): correlators = lax.psum(partial_traces, 'space') / nvec  30 us
    select_n x4, other arithmetic, phase_weights(): jnp.where(turns == 0, base_re, jnp.where(turns == 1, base_im, jnp.where(t...  23.8 us
    dot_general x4, matrix products, one_block(): left = jnp.dot(weight_re, stacked, preferred_element_type=jnp.float32)  18.3 us
    dot_general x4, matrix products, one_block(): right = jnp.dot(weight_im, stacked, preferred_element_type=jnp.float32)  6.29 us
    unnamed x13, local copies, waits for them, and re-layouts  5.89 us
    eq x4, other arithmetic, phase_weights(): turns == 0  5.79 us
    all_gather x1, blocking collectives, local(): every_slice = lax.all_gather(mesons, 'tm', axis=0, tiled=True)  5.42 us
  transfers between devices with their start and end apart: 1, of which 1 were waited for; matrix products, arithmetic and copies ran while one was open for 0% of the time, Pallas kernels for 0%

commit v1 on v0

v1 whole, which is shorter than its diff:
```python
import functools
import math

import jax
import jax.numpy as jnp
from jax import lax
from jax.experimental import pallas as pl
from jax.experimental.pallas import tpu as pltpu
from jax.sharding import PartitionSpec as P

EXTENT = 48
QC = 4
MESH = pl.DeviceIdType.MESH


def phases(momenta, offset, sites, rows):
    glob = offset + jnp.arange(sites, dtype=jnp.int32)
    coords = (glob % EXTENT, glob // EXTENT % EXTENT, glob // (EXTENT * EXTENT))
    qdotx = (
        momenta[:, 0:1] * coords[0][None, :]
        + momenta[:, 1:2] * coords[1][None, :]
        + momenta[:, 2:3] * coords[2][None, :]
    )
    angle = (qdotx % EXTENT).astype(jnp.float32) * jnp.float32(2.0 * math.pi / EXTENT)
    base_re = jnp.cos(angle).astype(jnp.bfloat16)
    base_im = (-jnp.sin(angle)).astype(jnp.bfloat16)
    both = jnp.stack([base_re, base_im], 0).astype(jnp.float32)
    return jnp.pad(both, ((0, 0), (0, rows - momenta.shape[0]), (0, 0)))


def kernel(dims, base_ref, noise_hbm, sol_hbm, mes_ref, tr_ref,
           raw, sol, nre, nim, acc, sbuf, hbuf, qbuf, rcore, ry, rz, xb, ps,
           in_sem, cs, cr, ys, yr, zs, zr, xs, xr, pss, psr):
    nspace, nslices, nchunks, rows, nvec, spincol, scale = dims
    nz = nspace // 4
    me = lax.axis_index("space")
    slice_id = lax.axis_index("tm")
    core = lax.rem(me, 2)
    yy = lax.rem(me // 2, 2)
    zz = me // 4

    barrier = pltpu.get_barrier_semaphore()
    for o in range(1, nspace):
        pl.semaphore_signal(barrier, inc=1, device_id={"space": lax.rem(me + o, nspace)}, device_id_type=MESH)
    for o in range(1, nslices):
        pl.semaphore_signal(barrier, inc=1, device_id={"tm": lax.rem(slice_id + o, nslices)}, device_id_type=MESH)

    noise_copy = pltpu.make_async_copy(noise_hbm, raw, in_sem.at[0])
    sol_copy = pltpu.make_async_copy(sol_hbm, sol, in_sem.at[1])
    noise_copy.start()
    sol_copy.start()
    noise_copy.wait()

    def turn(a, carry):
        k = raw[:, a, :]
        one = jnp.float32(1.0)
        zero = jnp.float32(0.0)
        re = jnp.where(k == 0, one, jnp.where(k == 2, -one, zero))
        im = jnp.where(k == 3, one, jnp.where(k == 1, -one, zero))
        nre[a] = re.astype(jnp.bfloat16)
        nim[a] = im.astype(jnp.bfloat16)
        return carry

    for a in range(spincol):
        turn(a, 0)
    sol_copy.wait()

    lane = lax.broadcasted_iota(jnp.int32, (QC * nvec, 2 * nvec), 1)
    sign = jnp.where(lane < nvec, jnp.float32(-1.0), jnp.float32(1.0))
    lane_r = lax.broadcasted_iota(jnp.int32, (nchunks * QC * rows, 2 * nvec), 1)
    sign_r = jnp.where(lane_r < nvec, jnp.float32(-1.0), jnp.float32(1.0))

    def compute(c):
        acc[...] = jnp.zeros_like(acc)
        sites = base_ref.shape[2]

        def body(a, carry):
            wre, wim = [], []
            n_r, n_i = nre[a], nim[a]
            for qq in range(QC):
                q = c * QC + qq
                br = jnp.broadcast_to(base_ref[0, pl.ds(q, 1), :], (nvec, sites)).astype(jnp.bfloat16)
                bi = jnp.broadcast_to(base_ref[1, pl.ds(q, 1), :], (nvec, sites)).astype(jnp.bfloat16)
                wre.append(n_r * br - n_i * bi)
                wim.append(n_r * bi + n_i * br)
            w = jnp.concatenate(wre + wim, axis=0)
            acc[...] += jnp.dot(w, sol[a], preferred_element_type=jnp.float32)
            return carry

        lax.fori_loop(0, spincol, body, 0)
        left = acc[: QC * nvec, :]
        right = acc[QC * nvec:, :]
        field = left + pltpu.roll(right, nvec, 1) * sign
        for qq in range(QC):
            for d in range(nspace):
                first = qq * nvec + d * rows
                sbuf[c, d % 2, (d // 2) % 2, d // 4, qq * rows:(qq + 1) * rows, :] = field[first:first + rows, :]

    def remote(src, dst, ssem, rsem, where):
        return pltpu.make_async_remote_copy(src_ref=src, dst_ref=dst, send_sem=ssem, recv_sem=rsem,
                                            device_id=where, device_id_type=MESH)

    core_peer = {"space": me + 1 - 2 * core}
    y_peer = {"space": me + 2 - 4 * yy}

    def core_copy(c):
        return remote(sbuf.at[c, 1 - core], rcore.at[c], cs.at[c], cr.at[c], core_peer)

    def y_copy(c):
        return remote(hbuf.at[c, 1 - yy], ry.at[c], ys.at[c], yr.at[c], y_peer)

    def z_copy(c, o):
        to = lax.rem(zz + o, nz)
        return remote(qbuf.at[c, to], rz.at[c, o - 1], zs.at[c, o - 1], zr.at[c, o - 1],
                      {"space": to * 4 + yy * 2 + core})

    def x_copy(c, o):
        return remote(xb.at[slice_id, c], xb.at[slice_id, c], xs.at[c, o - 1], xr.at[c, o - 1],
                      {"tm": lax.rem(slice_id + o, nslices)})

    def p_copy(o):
        return remote(ps.at[me], ps.at[me], pss.at[o - 1], psr.at[o - 1],
                      {"space": lax.rem(me + o, nspace)})

    for step in range(nchunks + 3):
        c = step
        if c < nchunks:
            compute(c)
            if c == 0:
                pl.semaphore_wait(barrier, nspace - 1 + nslices - 1)
            core_copy(c).start()
        c = step - 1
        if 0 <= c < nchunks:
            core_copy(c).wait_recv()
            hbuf[c, 1 - yy] = sbuf[c, core, 1 - yy] + rcore[c, 1 - yy]
            y_copy(c).start()
            hbuf[c, yy] = sbuf[c, core, yy] + rcore[c, yy]
        c = step - 2
        if 0 <= c < nchunks:
            y_copy(c).wait_recv()
            qbuf[c] = hbuf[c, yy] + ry[c]
            for o in range(1, nz):
                z_copy(c, o).start()
        c = step - 3
        if 0 <= c < nchunks:
            for o in range(1, nz):
                z_copy(c, o).wait_recv()
            total = qbuf[c, zz]
            for o in range(1, nz):
                total = total + rz[c, o - 1]
            total = total * jnp.float32(scale)
            xb[slice_id, c] = total
            mes_ref[c] = total
            for o in range(1, nslices):
                x_copy(c, o).start()

    for c in range(nchunks):
        for o in range(1, nslices):
            x_copy(c, o).wait_recv()

    lq = nchunks * QC * rows
    trows = ps.shape[1]
    rowid = lax.broadcasted_iota(jnp.int32, (trows, 2 * nvec), 0)
    found = jnp.zeros((trows, lq), jnp.float32)

    def add(found, row, prod):
        pick = jnp.where(rowid == row, jnp.float32(1.0), jnp.float32(0.0))
        return found + lax.dot_general(pick, prod, (((1,), (1,)), ((), ())), precision=lax.Precision.HIGHEST,
                                       preferred_element_type=jnp.float32)

    for w in range(nslices):
        mw = xb[w].reshape(lq, 2 * nvec)
        for u in range(w + 1):
            mu = xb[u].reshape(lq, 2 * nvec)
            found = add(found, w * nslices + u, mw * mu)
            if u < w:
                found = add(found, u * nslices + w, mw * (pltpu.roll(mu, nvec, 1) * sign_r))
    ps[me] = jnp.zeros(ps.shape[1:], jnp.float32)
    ps[me, :, :lq] = found
    for o in range(1, nspace):
        p_copy(o).start()
    for o in range(1, nspace):
        p_copy(o).wait_recv()
    total = ps[0]
    for d in range(1, nspace):
        total = total + ps[d]
    tr_ref[...] = total

    for c in range(nchunks):
        core_copy(c).wait_send()
        y_copy(c).wait_send()
        for o in range(1, nz):
            z_copy(c, o).wait_send()
        for o in range(1, nslices):
            x_copy(c, o).wait_send()
    for o in range(1, nspace):
        p_copy(o).wait_send()


def local(solutions, noise, momenta, pairs):
    _, spincol, sites, width = solutions.shape
    nvec = width // 2
    moms = momenta.shape[0]
    nspace = lax.axis_size("space")
    nslices = lax.axis_size("tm")
    nz = nspace // 4
    rows = nvec // nspace
    nchunks = -(-moms // QC)
    scale = 1.0 / math.sqrt(spincol * sites * nspace)
    offset = lax.axis_index("space") * sites
    base = phases(momenta, offset, sites, -(-nchunks * QC // 8) * 8)
    trows = -(-nslices * nslices // 8) * 8
    lq = nchunks * QC * rows
    lpad = -(-lq // 128) * 128
    dims = (nspace, nslices, nchunks, rows, nvec, spincol, scale)
    f32 = jnp.float32
    blk = (QC * rows, width)
    dma = pltpu.SemaphoreType.DMA
    vmem = pl.BlockSpec(memory_space=pltpu.VMEM)
    hbm = pl.BlockSpec(memory_space=pl.ANY)
    mes, traces = pl.pallas_call(
        functools.partial(kernel, dims),
        out_shape=(jax.ShapeDtypeStruct((nchunks,) + blk, f32), jax.ShapeDtypeStruct((trows, lpad), f32)),
        in_specs=[vmem, hbm, hbm],
        out_specs=(vmem, vmem),
        scratch_shapes=[
            pltpu.VMEM((nvec, spincol, sites), jnp.int32),
            pltpu.VMEM((spincol, sites, width), jnp.bfloat16),
            pltpu.VMEM((spincol, nvec, sites), jnp.bfloat16),
            pltpu.VMEM((spincol, nvec, sites), jnp.bfloat16),
            pltpu.VMEM((2 * QC * nvec, width), f32),
            pltpu.VMEM((nchunks, 2, 2, nz) + blk, f32),
            pltpu.VMEM((nchunks, 2, nz) + blk, f32),
            pltpu.VMEM((nchunks, nz) + blk, f32),
            pltpu.VMEM((nchunks, 2, nz) + blk, f32),
            pltpu.VMEM((nchunks, nz) + blk, f32),
            pltpu.VMEM((nchunks, nz - 1) + blk, f32),
            pltpu.VMEM((nslices, nchunks) + blk, f32),
            pltpu.VMEM((nspace, trows, lpad), f32),
            dma((2,)),
            dma((nchunks,)), dma((nchunks,)),
            dma((nchunks,)), dma((nchunks,)),
            dma((nchunks, nz - 1)), dma((nchunks, nz - 1)),
            dma((nchunks, nslices - 1)), dma((nchunks, nslices - 1)),
            dma((nspace - 1,)), dma((nspace - 1,)),
        ],
        compiler_params=pltpu.CompilerParams(collective_id=0, has_side_effects=True, vmem_limit_bytes=60 * 2**20),
    )(base, noise[0], solutions[0])
    mesons = mes.reshape(nchunks * QC, rows, 2, nvec)[:moms].transpose(2, 0, 1, 3)[None]
    table = jnp.sum(traces[:, :lq].reshape(trows, nchunks * QC, rows), axis=2)[:, :moms] / nvec
    source, sink = pairs[:, 0], pairs[:, 1]
    high, low = jnp.maximum(source, sink), jnp.minimum(source, sink)
    slots = jnp.arange(trows, dtype=jnp.int32)

    def pick(index):
        return jnp.sum(jnp.where((index[:, None] == slots[None, :])[:, :, None], table[None], 0.0), axis=1)

    real = pick(high * nslices + low)
    imag = pick(low * nslices + high)
    imag = jnp.where((sink > source)[:, None], imag, jnp.where((sink < source)[:, None], -imag, 0.0))
    return (mesons, jnp.stack([real, imag], 1))


def solution(mesh):
    in_specs = (P("tm", None, "space", None), P("tm", None, None, "space"), P(), P("tm", None))
    out_specs = (P("tm", None, None, "space", None), P("tm", None, None))
    return jax.shard_map(local, mesh=mesh, in_specs=in_specs, out_specs=out_specs, check_vma=False)
```

time: 224 us -> 64.6 us (0.29)
  waiting for transfers between devices: 98.4 us -> 0 us
  Pallas kernels: 0 us -> 54.6 us
  blocking collectives: 35.4 us -> 0 us
  other arithmetic: 35.8 us -> 1.4 us
  matrix products: 25.9 us -> 0 us
  between operations: 14.8 us -> 0.69 us
  local copies, waits for them, and re-layouts: 12.7 us -> 7.58 us
    unnamed x2 -> x0, waiting for transfers between devices: 98.4 us -> none
    pallas_call x0 -> x1, Pallas kernels: none -> 54.6 us  [local(): pl.pallas_call(functools.partial(kernel, dims), out_shape=(jax.ShapeDtype...]
    psum x1 -> x0, blocking collectives: 30 us -> none  [local(): correlators = lax.psum(partial_traces, 'space') / nvec]
    dot_general x10 -> x0, matrix products: 25.9 us -> none  [the longest x4 18.3 us: one_block(): left = jnp.dot(weight_re, stacked, preferred_element_type=jnp.float32)]
    select_n x12 -> x3, other arithmetic: 24 us -> 0.11 us  [the longest x1 0.07 us: local(): jnp.where((sink > source)[:, None], imag, jnp.where((sink < source)[:, No...]
    eq x4 -> x1, other arithmetic: 5.79 us -> 0.08 us  [pick(): index[:, None] == slots[None, :]]
    all_gather x1 -> x0, blocking collectives: 5.42 us -> none  [local(): every_slice = lax.all_gather(mesons, 'tm', axis=0, tiled=True)]
    dynamic_slice x4 -> x0, local copies, waits for them, and re-layouts: 4.09 us -> none  [one_block(): vec_block = lax.dynamic_slice_in_dim(vectors, first, block, 1)]
  transfers between devices with their start and end apart: 1 -> 0, of which waited for: 1 -> 0; matrix products, arithmetic and copies ran while one was open for 0% -> 0% of each run, Pallas kernels for 0% -> 0%
where the time goes in v1:
time: 64.6 us; the launch traced here: 64.3 us
  Pallas kernels  54.6 us (85%)
  local copies, waits for them, and re-layouts  7.58 us (12%)
  other arithmetic  1.4 us (2%)
  between operations  0.69 us (1%)
    pallas_call x1, Pallas kernels, local(): pl.pallas_call(functools.partial(kernel, dims), out_shape=(jax.ShapeDtype...  54.6 us
    unnamed x6, local copies, waits for them, and re-layouts  5.06 us

profile of v1, /device:TPU:0, one launch (start us, length us, event | category | flops | bytes accessed | tf_op | source)
XLA Modules:
  0.0 64.3 jit_solution(2342858643847426946)
XLA Ops:
  0.7 0.8 %slice_bitcast_fusion.2 = (s32[27]{0:T(128)S(1)}, s32[27]{0:T(128)S(1)}, s32[27]{0:T(128)S(1)}) fusion(s32[27,3]{0,1:T(4,128)} %param.6), kind=kLoop, calls=%fused_computation.44 | loop fusion | bytes 648 | tf_op jit(solution)/shard_map/mul | solution.py:20
  1.5 0.4 cosine_convert_fusion
  1.8 0.7 %fusion.5.base_ref = f32[2,32,512]{2,1,0:T(8,128)} fusion(bf16[1,27,512]{2,1,0:T(8,128)(2,1)S(1)} %get-tuple-element.13, bf16[1,27,512]{2,1,0:T(8,128)(2,1)S(1)} %get-tuple-element.12), kind=kLoop, calls=%fused_computation.9 | loop fusion | flops 229376 | bytes 186368 | tf_op jit(solution)/shard_map/jit(_pad)/pad | solution.py:28
  2.5 3.7 %copy.29 = s32[1,64,12,512]{3,2,1,0:T(8,128)} copy(s32[1,64,12,512]{3,1,2,0:T(8,128)} %param.5) | data formatting | bytes 3145728 | tf_op args[1]
  6.2 0.0 copy-start
  6.2 54.6 %shard_map.59 = (f32[7,16,128]{2,1,0:T(8,128)}, f32[8,128]{1,0:T(8,128)}) custom-call(f32[2,32,512]{2,1,0:T(8,128)} %fusion.5.base_ref, s32[64,12,512]{2,1,0:T(8,128)} %bitcast.34, bf16[12,512,128]{2,1,0:T(8,128)(2,1)} %bitcast.35), custom_call_target="tpu_custom_call" | custom-call | tf_op jit(solution)/shard_map/pallas_call | solution.py:221
  60.9 0.8 %copy.22 = f32[8,112]{0,1:T(8,128)S(1)} copy(f32[8,112]{1,0:T(8,128)} %bitcast.40) | data formatting | bytes 7168 | tf_op jit(solution)/shard_map/slice | solution.py:250
  61.7 0.1 copy.26
  61.8 0.0 copy-done
  61.8 0.1 iota_compare_fusion.1
  61.9 0.1 select_reduce_fusion.1
  62.0 0.1 bitcast_select_fusion
  62.1 0.6 copy.24
  62.7 0.9 %reshape.496 = f32[28,4,2,64]{3,2,1,0:T(2,128)S(1)} reshape(f32[7,16,128]{2,1,0:T(8,128)} %get-tuple-element.4) | data formatting | bytes 114688 | tf_op jit(solution)/shard_map/reshape | solution.py:249
  63.6 0.7 %copy.30 = f32[27,4,2,64]{3,1,0,2:T(4,128)} copy(f32[27,4,2,64]{3,2,1,0:T(2,128)S(1)} %slice.32) | data formatting | bytes 110592
  (8 shorter events, 0.1 us)
Async XLA Ops:
  6.2 55.6 %copy-start = (s32[8,2]{0,1:T(2,128)S(1)}, s32[8,2]{0,1:T(2,128)}, u32[]{:S(2)}) copy-start(s32[8,2]{0,1:T(2,128)} %param.7) | copy-start | bytes 196

commit v2 on v1

--- a/solution.py
+++ b/solution.py
@@ -10,26 +10,38 @@
 
 EXTENT = 48
 QC = 4
+GROUP = 2
 MESH = pl.DeviceIdType.MESH
 
 
-def phases(momenta, offset, sites, rows):
-    glob = offset + jnp.arange(sites, dtype=jnp.int32)
-    coords = (glob % EXTENT, glob // EXTENT % EXTENT, glob // (EXTENT * EXTENT))
-    qdotx = (
-        momenta[:, 0:1] * coords[0][None, :]
-        + momenta[:, 1:2] * coords[1][None, :]
-        + momenta[:, 2:3] * coords[2][None, :]
-    )
-    angle = (qdotx % EXTENT).astype(jnp.float32) * jnp.float32(2.0 * math.pi / EXTENT)
-    base_re = jnp.cos(angle).astype(jnp.bfloat16)
-    base_im = (-jnp.sin(angle)).astype(jnp.bfloat16)
-    both = jnp.stack([base_re, base_im], 0).astype(jnp.float32)
-    return jnp.pad(both, ((0, 0), (0, rows - momenta.shape[0]), (0, 0)))
-
-
-def kernel(dims, base_ref, noise_hbm, sol_hbm, mes_ref, tr_ref,
-           raw, sol, nre, nim, acc, sbuf, hbuf, qbuf, rcore, ry, rz, xb, ps,
+def wrap(value):
+    return jnp.floor((value + 0.5) * jnp.float32(1.0 / EXTENT))
+
+
+def column(ref, row):
+    size = ref.shape[1]
+    here = lax.broadcasted_iota(jnp.int32, (size, size), 0)
+    there = lax.broadcasted_iota(jnp.int32, (size, size), 1)
+    line = jnp.broadcast_to(ref[row:row + 1, :].astype(jnp.float32), (size, size))
+    return jnp.sum(jnp.where(here == there, line, jnp.float32(0.0)), axis=1, keepdims=True)
+
+
+def phases(mom_ref, offset, sites):
+    moms = mom_ref.shape[1]
+    glob = (lax.broadcasted_iota(jnp.int32, (moms, sites), 1) + offset).astype(jnp.float32)
+    line = wrap(glob)
+    plane = wrap(line)
+    xx = glob - line * EXTENT
+    yy = line - plane * EXTENT
+    dot = column(mom_ref, 0) * xx + column(mom_ref, 1) * yy + column(mom_ref, 2) * plane
+    angle = (dot - wrap(dot) * EXTENT) * jnp.float32(2.0 * math.pi / EXTENT)
+    base_re = jnp.cos(angle).astype(jnp.bfloat16).astype(jnp.float32)
+    base_im = (-jnp.sin(angle)).astype(jnp.bfloat16).astype(jnp.float32)
+    return base_re, base_im
+
+
+def kernel(dims, mom_ref, pair_ref, noise_hbm, sol_hbm, mes_ref, tr_ref,
+           base_ref, raw, sol, nre, nim, acc, sbuf, hbuf, qbuf, rcore, ry, rz, xb, ps,
            in_sem, cs, cr, ys, yr, zs, zr, xs, xr, pss, psr):
     nspace, nslices, nchunks, rows, nvec, spincol, scale = dims
     nz = nspace // 4
@@ -49,10 +61,15 @@
     sol_copy = pltpu.make_async_copy(sol_hbm, sol, in_sem.at[1])
     noise_copy.start()
     sol_copy.start()
+    moms = mom_ref.shape[1]
+    base_re, base_im = phases(mom_ref, me * sol.shape[1], sol.shape[1])
+    base_ref[...] = jnp.zeros_like(base_ref)
+    base_ref[0, :moms] = base_re
+    base_ref[1, :moms] = base_im
     noise_copy.wait()
 
     def turn(a, carry):
-        k = raw[:, a, :]
+        k = raw[a]
         one = jnp.float32(1.0)
         zero = jnp.float32(0.0)
         re = jnp.where(k == 0, one, jnp.where(k == 2, -one, zero))
@@ -74,20 +91,25 @@
         acc[...] = jnp.zeros_like(acc)
         sites = base_ref.shape[2]
 
-        def body(a, carry):
-            wre, wim = [], []
-            n_r, n_i = nre[a], nim[a]
-            for qq in range(QC):
-                q = c * QC + qq
-                br = jnp.broadcast_to(base_ref[0, pl.ds(q, 1), :], (nvec, sites)).astype(jnp.bfloat16)
-                bi = jnp.broadcast_to(base_ref[1, pl.ds(q, 1), :], (nvec, sites)).astype(jnp.bfloat16)
-                wre.append(n_r * br - n_i * bi)
-                wim.append(n_r * bi + n_i * br)
-            w = jnp.concatenate(wre + wim, axis=0)
-            acc[...] += jnp.dot(w, sol[a], preferred_element_type=jnp.float32)
+        def body(step, carry):
+            columns = []
+            for k in range(GROUP):
+                a = step * GROUP + k
+                wre, wim = [], []
+                n_r, n_i = nre[a], nim[a]
+                for qq in range(QC):
+                    q = c * QC + qq
+                    br = jnp.broadcast_to(base_ref[0, pl.ds(q, 1), :].astype(jnp.bfloat16), (nvec, sites))
+                    bi = jnp.broadcast_to(base_ref[1, pl.ds(q, 1), :].astype(jnp.bfloat16), (nvec, sites))
+                    wre.append(n_r * br - n_i * bi)
+                    wim.append(n_r * bi + n_i * br)
+                columns.append(jnp.concatenate(wre + wim, axis=0))
+            w = jnp.concatenate(columns, axis=1)
+            v = sol[pl.ds(step * GROUP, GROUP)].reshape(GROUP * sites, 2 * nvec)
+            acc[...] += jnp.dot(w, v, preferred_element_type=jnp.float32)
             return carry
 
-        lax.fori_loop(0, spincol, body, 0)
+        lax.fori_loop(0, spincol // GROUP, body, 0)
         left = acc[: QC * nvec, :]
         right = acc[QC * nvec:, :]
         field = left + pltpu.roll(right, nvec, 1) * sign
@@ -150,7 +172,10 @@
                 total = total + rz[c, o - 1]
             total = total * jnp.float32(scale)
             xb[slice_id, c] = total
-            mes_ref[c] = total
+            for qq in range(min(QC, moms - c * QC)):
+                part = total[qq * rows:(qq + 1) * rows, :]
+                mes_ref[0, c * QC + qq] = part[:, :nvec]
+                mes_ref[1, c * QC + qq] = part[:, nvec:]
             for o in range(1, nslices):
                 x_copy(c, o).start()
 
@@ -184,7 +209,24 @@
     total = ps[0]
     for d in range(1, nspace):
         total = total + ps[d]
-    tr_ref[...] = total
+    lpad = total.shape[1]
+    left_id = lax.broadcasted_iota(jnp.int32, (lpad, 128), 0)
+    first = lax.broadcasted_iota(jnp.int32, (lpad, 128), 1) * rows
+    fold = jnp.where((left_id >= first) & (left_id < first + rows), jnp.float32(1.0), jnp.float32(0.0))
+
+    def exact_dot(p, r):
+        return jnp.dot(p, r, precision=lax.Precision.HIGHEST, preferred_element_type=jnp.float32)
+
+    table = exact_dot(total, fold) * jnp.float32(1.0 / nvec)
+    source, sink = column(pair_ref, 0).astype(jnp.int32), column(pair_ref, 1).astype(jnp.int32)
+    high, low = jnp.maximum(source, sink), jnp.minimum(source, sink)
+    slot = lax.broadcasted_iota(jnp.int32, (pair_ref.shape[1], trows), 1)
+    one, zero = jnp.float32(1.0), jnp.float32(0.0)
+    turned = jnp.where(sink > source, one, jnp.where(sink < source, -one, zero))
+    real = exact_dot(jnp.where(slot == high * nslices + low, one, zero), table)
+    imag = exact_dot(jnp.where(slot == low * nslices + high, turned, zero), table)
+    tr_ref[:, 0, :] = real[:, :moms]
+    tr_ref[:, 1, :] = imag[:, :moms]
 
     for c in range(nchunks):
         core_copy(c).wait_send()
@@ -207,8 +249,6 @@
     rows = nvec // nspace
     nchunks = -(-moms // QC)
     scale = 1.0 / math.sqrt(spincol * sites * nspace)
-    offset = lax.axis_index("space") * sites
-    base = phases(momenta, offset, sites, -(-nchunks * QC // 8) * 8)
     trows = -(-nslices * nslices // 8) * 8
     lq = nchunks * QC * rows
     lpad = -(-lq // 128) * 128
@@ -218,13 +258,15 @@
     dma = pltpu.SemaphoreType.DMA
     vmem = pl.BlockSpec(memory_space=pltpu.VMEM)
     hbm = pl.BlockSpec(memory_space=pl.ANY)
-    mes, traces = pl.pallas_call(
+    mesons, correlators = pl.pallas_call(
         functools.partial(kernel, dims),
-        out_shape=(jax.ShapeDtypeStruct((nchunks,) + blk, f32), jax.ShapeDtypeStruct((trows, lpad), f32)),
-        in_specs=[vmem, hbm, hbm],
+        out_shape=(jax.ShapeDtypeStruct((2, moms, rows, nvec), f32),
+                   jax.ShapeDtypeStruct((pairs.shape[0], 2, moms), f32)),
+        in_specs=[vmem, vmem, hbm, hbm],
         out_specs=(vmem, vmem),
         scratch_shapes=[
-            pltpu.VMEM((nvec, spincol, sites), jnp.int32),
+            pltpu.VMEM((2, -(-nchunks * QC // 8) * 8, sites), f32),
+            pltpu.VMEM((spincol, nvec, sites), jnp.int32),
             pltpu.VMEM((spincol, sites, width), jnp.bfloat16),
             pltpu.VMEM((spincol, nvec, sites), jnp.bfloat16),
             pltpu.VMEM((spincol, nvec, sites), jnp.bfloat16),
@@ -245,20 +287,8 @@
             dma((nspace - 1,)), dma((nspace - 1,)),
         ],
         compiler_params=pltpu.CompilerParams(collective_id=0, has_side_effects=True, vmem_limit_bytes=60 * 2**20),
-    )(base, noise[0], solutions[0])
-    mesons = mes.reshape(nchunks * QC, rows, 2, nvec)[:moms].transpose(2, 0, 1, 3)[None]
-    table = jnp.sum(traces[:, :lq].reshape(trows, nchunks * QC, rows), axis=2)[:, :moms] / nvec
-    source, sink = pairs[:, 0], pairs[:, 1]
-    high, low = jnp.maximum(source, sink), jnp.minimum(source, sink)
-    slots = jnp.arange(trows, dtype=jnp.int32)
-
-    def pick(index):
-        return jnp.sum(jnp.where((index[:, None] == slots[None, :])[:, :, None], table[None], 0.0), axis=1)
-
-    real = pick(high * nslices + low)
-    imag = pick(low * nslices + high)
-    imag = jnp.where((sink > source)[:, None], imag, jnp.where((sink < source)[:, None], -imag, 0.0))
-    return (mesons, jnp.stack([real, imag], 1))
+    )(momenta.T, pairs.T, noise[0].transpose(1, 0, 2), solutions[0])
+    return (mesons[None], correlators)
 
 
 def solution(mesh):

time: 64.6 us -> 48.6 us (0.75)
  Pallas kernels: 54.6 us -> 44.9 us
  local copies, waits for them, and re-layouts: 7.58 us -> 2.84 us
  other arithmetic: 1.4 us -> 0 us
    pallas_call x1, Pallas kernels: 54.6 us -> 44.9 us  [local(): pl.pallas_call(functools.partial(kernel, dims), out_shape=(jax.ShapeDtype...]
    unnamed x6 -> x2, local copies, waits for them, and re-layouts: 5.06 us -> 2.84 us
    reshape x1 -> x0, local copies, waits for them, and re-layouts: 0.94 us -> none  [local(): mes.reshape(nchunks * QC, rows, 2, nvec)[:moms].transpose(2, 0, 1, 3)[None]]
    mul x1 -> x0, local copies, waits for them, and re-layouts: 0.8 us -> none  [phases(): momenta[:, 0:1] * coords[0][None, :] + momenta[:, 1:2] * coords[1][None, :]]
    slice x2 -> x0, local copies, waits for them, and re-layouts: 0.79 us -> none  [the longest x1 0.78 us: local(): traces[:, :lq].reshape(trows, nchunks * QC, rows)]
    pad x1 -> x0, other arithmetic: 0.68 us -> none  [phases(): return jnp.pad(both, ((0, 0), (0, rows - momenta.shape[0]), (0, 0)))]
where the time goes in v2:
time: 48.6 us; the launch traced here: 48.4 us
  Pallas kernels  44.9 us (92%)
  local copies, waits for them, and re-layouts  2.84 us (6%)
  between operations  0.64 us (1%)
    pallas_call x1, Pallas kernels, local(): pl.pallas_call(functools.partial(kernel, dims), out_shape=(jax.ShapeDtype...  44.9 us
    unnamed x2, local copies, waits for them, and re-layouts  2.84 us

profile of v2, /device:TPU:0, one launch (start us, length us, event | category | flops | bytes accessed | tf_op | source)
XLA Modules:
  0.0 48.4 jit_solution(13348930596025271150)
XLA Ops:
  0.6 44.9 %shard_map.59 = (f32[2,27,4,64]{3,2,1,0:T(4,128)}, f32[8,2,27]{2,1,0:T(2,128)}) custom-call(s32[3,27]{1,0:T(4,128)} %bitcast.10, s32[2,8]{1,0:T(2,128)} %bitcast.11, s32[12,64,512]{2,1,0:T(8,128)} %bitcast.7, bf16[12,512,128]{2,1,0:T(8,128)(2,1)} %bitcast.8), custom_call_target="tpu_custom_call" | custom-call | tf_op jit(solution)/shard_map/pallas_call | solution.py:261
  45.6 1.5 %copy.8 = f32[1,2,27,4,64]{4,3,2,1,0:T(4,128)} copy(f32[1,2,27,4,64]{4,3,2,1,0:T(4,128)} %bitcast.9) | data formatting | bytes 110592
  47.1 1.3 %copy.9 = f32[8,2,27]{2,1,0:T(2,128)} copy(f32[8,2,27]{2,1,0:T(2,128)} %get-tuple-element.9) | data formatting | bytes 3456
